TPU v7x, 32 devices: a whole 2x2x4 slice. The times are simulated.
32 devices in a mesh: node: 8 (over y, x, core), local: 4 (over z).
Axes of the slice: x: 2, y: 2, z: 4, core: 2. Of those that a mesh axis runs over, the one named last changes fastest.
Arguments:
- vit_tiles: bfloat16 [8, 4, 128, 12800], P('node', 'local'), may hold values from -6 to 6
- tile_counts: int32 [8, 1], P('node'), may hold values from 1 to 2
- block_of_piece: int32 [8, 2], P('node'), may hold values from 0 to 7, as said below
- segment_ids: int32 [8, 8, 256], P('node', None, 'local'), may hold values from 0 to 15, as said below
- text_rows: bfloat16 [8, 8, 256, 3584], P('node', None, 'local'), may hold values from -6 to 6
- cotangent: bfloat16 [8, 8, 256, 512], P('node', None, 'local'), may hold values from -6 to 6
- proj_weight: bfloat16 [12800, 3584], P('local', 'node'), may hold values from -0.0546875 to 0.0546875
- proj_bias: float32 [3584], replicated, may hold values from -3 to 3
- out_weight: bfloat16 [3584, 3584], P(None, 'local'), may hold values from -0.09375 to 0.09375
- out_bias: float32 [3584], replicated, may hold values from -3 to 3
- ln_gain: float32 [12800], replicated, may hold values from 0.25 to 1.75
- ln_bias: float32 [12800], replicated, may hold values from -2 to 2
- norm_gain: float32 [3584], replicated, may hold values from 0.25 to 1.75
- v_weight: bfloat16 [3584, 512], P(('node', 'local')), may hold values from -0.09375 to 0.09375
Outputs:
- hidden_grad: bfloat16 [8, 8, 256, 3584], P('node', None, 'local')
- value_weight_grad: float32 [3584, 512], P(('node', 'local'))
- value_bias_grad: float32 [512], replicated
- norm_gain_grad: float32 [3584], replicated
Inputs may be any that keep to these rules, and one draw needn't show every extreme that they name: `block_of_piece`: within one sequence the entries are distinct. `segment_ids`: along each sequence, read block by block, the ids never fall; every sequence has exactly 16 documents.
All inputs are finite; a program needn't handle non-finite values.
Results may differ from a plain program's by a relative error of at most 0.017.
Values may be sent and summed in bfloat16 or wider, within the bound.
A program may use at most 128 MiB of HBM per device.

v0:
```python
import jax
import jax.numpy as jnp
from jax import lax
from jax.sharding import PartitionSpec as P

SLOTS = 2
DOCS = 16


def layer_norm(vit_rows, scale_vec, shift_vec):
    values = vit_rows.astype(jnp.float32)
    average = jnp.mean(values, -1, keepdims=True)
    centred = values - average
    variance = jnp.mean(centred * centred, -1, keepdims=True)
    return (centred * lax.rsqrt(variance + 1e-05) * scale_vec + shift_vec).astype(jnp.bfloat16)


def per_device(
    vit_tiles,
    tile_counts,
    block_of_piece,
    segment_ids,
    text_rows,
    cotangent,
    proj_weight,
    proj_bias,
    out_weight,
    out_bias,
    ln_gain,
    ln_bias,
    norm_gain,
    v_weight,
):
    local_count = lax.axis_size("local")
    node_count = lax.axis_size("node")
    own_index = lax.axis_index("local")
    blocks = text_rows.shape[1]
    share_rows = text_rows.shape[2]
    model_width = text_rows.shape[3]
    out_cols = out_weight.shape[1]
    normed = layer_norm(vit_tiles[0, 0], ln_gain, ln_bias)
    received = lax.all_to_all(normed, "local", split_axis=1, concat_axis=0, tiled=True)
    first_rows = lax.all_gather(proj_weight, "node", axis=1, tiled=True)
    bias_cols = lax.dynamic_slice_in_dim(out_bias, own_index * out_cols, out_cols, 0)
    term = jnp.dot(received, first_rows, preferred_element_type=jnp.float32)
    rounded = lax.optimization_barrier(term.astype(jnp.bfloat16))
    own_sum = lax.psum_scatter(
        rounded.astype(jnp.float32).astype(jnp.bfloat16), "local", scatter_dimension=0, tiled=True
    ).astype(jnp.float32)
    middle = jax.nn.gelu(own_sum + proj_bias, approximate=False).astype(jnp.bfloat16)
    columns_out = (
        jnp.dot(
            lax.all_gather(middle, "local", axis=0, tiled=True),
            out_weight,
            preferred_element_type=jnp.float32,
        )
        + bias_cols
    ).astype(jnp.bfloat16)
    run_rows = share_rows // 2
    columns_out = columns_out.reshape(local_count, local_count, run_rows, out_cols)
    arrived = lax.all_to_all(columns_out, "local", split_axis=1, concat_axis=3, tiled=True)
    piece_total = local_count // 2
    arrived = arrived.reshape(piece_total, share_rows, model_width)
    piece_ids = lax.iota(jnp.int32, piece_total)
    filled = piece_ids % SLOTS < jnp.repeat(tile_counts[0], SLOTS)
    chosen = (block_of_piece[0][None, :] == lax.iota(jnp.int32, blocks)[:, None]) & filled[None, :]
    placed = jnp.einsum(
        "bp,ptd->btd", chosen.astype(jnp.bfloat16), arrived, preferred_element_type=jnp.float32
    )
    is_image = jnp.any(chosen, 1)
    hidden = jnp.where(is_image[:, None, None], placed.astype(jnp.bfloat16), text_rows[0])
    hidden = hidden.reshape(blocks * share_rows, model_width)
    doc_ids = segment_ids[0].reshape(-1)
    doc_hits = (doc_ids[:, None] == lax.iota(jnp.int32, DOCS)[None, :]).astype(jnp.float32)
    doc_sizes = lax.psum(jnp.sum(doc_hits, 0), "local")
    doc_weight = blocks * share_rows * local_count / (DOCS * doc_sizes)
    token_weight = jnp.dot(doc_hits, doc_weight, precision=lax.Precision.HIGHEST)
    value_grad = (
        cotangent[0].reshape(-1, cotangent.shape[3]).astype(jnp.float32) * token_weight[:, None]
    ).astype(jnp.bfloat16)
    hidden_f = hidden.astype(jnp.float32)
    inv_rms = lax.rsqrt(jnp.mean(hidden_f * hidden_f, -1, keepdims=True) + 1e-06)
    normed_input = (hidden_f * inv_rms * norm_gain).astype(jnp.bfloat16)
    grad_normed = lax.dot_general(
        value_grad,
        lax.all_gather(v_weight, ("node", "local"), axis=0, tiled=True),
        (((1,), (1,)), ((), ())),
        preferred_element_type=jnp.float32,
    )
    gain_part = jnp.sum(grad_normed * hidden_f * inv_rms, 0)
    scaled = grad_normed * norm_gain
    grad_hidden = inv_rms * scaled - hidden_f * (inv_rms * inv_rms * inv_rms) * jnp.mean(
        scaled * hidden_f, -1, keepdims=True
    )
    bias_part = jnp.sum(value_grad.astype(jnp.float32), 0)
    rows_each = model_width // (node_count * local_count)
    reordered = (
        normed_input.reshape(-1, node_count, local_count, rows_each)
        .transpose(0, 2, 1, 3)
        .reshape(-1, model_width)
    )
    partial_sum = lax.psum_scatter(
        lax.dot_general(
            reordered, value_grad, (((0,), (0,)), ((), ())), preferred_element_type=jnp.float32
        ).astype(jnp.bfloat16),
        "local",
        scatter_dimension=0,
        tiled=True,
    )
    grad_weight = lax.psum_scatter(partial_sum, "node", scatter_dimension=0, tiled=True).astype(
        jnp.float32
    )
    grad_bias, grad_gain = lax.psum((bias_part, gain_part), ("node", "local"))
    grad_hidden = grad_hidden.astype(jnp.bfloat16).reshape(1, blocks, share_rows, model_width)
    return (grad_hidden, grad_weight / node_count, grad_bias / node_count, grad_gain / node_count)


def solution(mesh):
    in_specs = (
        P("node", "local", None, None),
        P("node", None),
        P("node", None),
        P("node", None, "local"),
        P("node", None, "local", None),
        P("node", None, "local", None),
        P("local", "node"),
        P(),
        P(None, "local"),
        P(),
        P(),
        P(),
        P(),
        P(("node", "local"), None),
    )
    out_specs = (P("node", None, "local", None), P(("node", "local"), None), P(), P())
    return jax.shard_map(
        per_device, mesh=mesh, in_specs=in_specs, out_specs=out_specs, check_vma=False
    )
```

profile of v0, /device:TPU:0, one launch (start us, length us, event | category | flops | bytes accessed | tf_op | source)
XLA Modules:
  0.0 511.1 jit_solution(9260454997335006705)
XLA Ops:
  7.2 0.7 all-gather.4.cloned.1.call-update
  8.0 4.3 copy.62
  12.3 1.7 convert_reduce_fusion
  14.1 1.7 fusion.7
  15.8 4.2 add_convert_fusion
  20.0 79.6 %all_to_all.31 = bf16[128,4,3200]{0,2,1:T(8,128)(2,1)S(1)} all-to-all(bf16[128,4,3200]{0,2,1:T(8,128)(2,1)S(1)} %add_convert_fusion), channel_id=1, replica_groups=mesh['node'=8,'local'=4] {'local'}, dimensions={1} | all-to-all | bytes 6553600 | tf_op jit(solution)/shard_map/all_to_all | solution.py:42
  99.6 3.5 copy.63
  103.1 25.3 %all-gather.4.cloned.1.call-done = bf16[3200,3584]{0,1:T(8,128)(2,1)} async-done(((bf16[3200,448]{0,1:T(8,128)(2,1)}), bf16[3200,3584]{0,1:T(8,128)(2,1)}) %all-gather.4.cloned.1.call-update) | async-done | bytes 22937616 | tf_op jit(solution)/shard_map/all_gather | solution.py:43
  128.4 19.2 %convolution_convert_fusion = bf16[512,3584]{1,0:T(8,128)(2,1)} fusion(bf16[512,3200]{1,0:T(8,128)(2,1)} %bitcast.68, bf16[3200,3584]{0,1:T(8,128)(2,1)} %all-gather.4.cloned.1.call-done), kind=kOutput, calls=%fused_computation.15 | convolution fusion | flops 11745886208 | bytes 29884416 | tf_op jit(solution)/shard_map/dot_general | solution.py:45
  147.6 0.0 all-gather.6.cloned.1.call-start
  147.6 68.6 %reduce-scatter.4.cloned.1.call-done = bf16[128,3584]{1,0:T(8,128)(2,1)} async-done(((bf16[512,3584]{1,0:T(8,128)(2,1)}), bf16[128,3584]{1,0:T(8,128)(2,1)}) %reduce-scatter.4.cloned.1.call-update) | async-done | bytes 917520 | tf_op jit(solution)/shard_map/reduce_scatter | solution.py:47
  216.3 5.8 %fusion.13 = bf16[128,3584]{1,0:T(8,128)(2,1)} fusion(bf16[128,3584]{1,0:T(8,128)(2,1)} %reduce-scatter.4.cloned.1.call-done, f32[3584]{0:T(1024)S(1)} %copy-done.4), kind=kLoop, calls=%fused_computation.25 | loop fusion | flops 30736384 | bytes 1849344 | tf_op jit(solution)/shard_map/convert_element_type | solution.py:50
  222.1 0.0 all-gather.8.cloned.1.call-start
  222.2 0.5 all-gather.8.cloned.1.call-update
  222.7 0.8 dynamic_slice.3
  223.5 71.2 %all-gather.6.cloned.1.call-done = bf16[512,3584]{1,0:T(8,128)(2,1)} async-done(((bf16[128,3584]{1,0:T(8,128)(2,1)}), bf16[512,3584]{1,0:T(8,128)(2,1)}) %all-gather.6.cloned.1.call-update) | async-done | bytes 3670032 | tf_op jit(solution)/shard_map/all_gather | solution.py:53
  294.6 7.9 %add_convert_fusion.1 = bf16[512,896]{1,0:T(8,128)(2,1)S(1)} fusion(bf16[512,3584]{1,0:T(8,128)(2,1)} %all-gather.6.cloned.1.call-done, bf16[3584,896]{1,0:T(8,128)(2,1)} %param.22, f32[896]{0:T(1024)S(1)} %dynamic_slice.3), kind=kOutput, calls=%fused_computation.26 | convolution fusion | flops 3289251840 | bytes 11013632 | tf_op jit(solution)/shard_map/dot_general | solution.py:52
  302.6 1.0 copy.64
  303.6 3.5 all-to-all-start.1
  307.8 0.1 eq.36
  307.9 0.1 convert_reduce_fusion.2
  308.0 21.8 %psum.21 = f32[16]{0:T(128)S(1)} all-reduce(f32[16]{0:T(128)S(1)} %convert_reduce_fusion.2), channel_id=1, replica_groups=mesh['node'=8,'local'=4] {'local'}, use_global_device_ids=true, to_apply=%region_6.7 | all-reduce | flops 16 | bytes 128 | tf_op jit(solution)/shard_map/psum | solution.py:75
  329.8 0.1 fusion.26
  330.0 0.1 mul.176
  330.0 0.1 mul.173
  330.2 0.1 fusion.29
  330.2 0.2 convert_reduce_fusion.1
  330.4 4.9 all-to-all-done.1
  335.4 0.7 copy.65
  336.1 0.3 reshape.145
  336.4 11.2 %multiply_reduce_fusion = (f32[8,64]{0,1:T(8,128)S(1)}, f32[8,64,3584]{2,0,1:T(8,128)}) fusion(bf16[1,8,64,3584]{3,2,1,0:T(8,128)(2,1)} %param.18, bf16[2,64,3584]{2,1,0:T(8,128)(2,1)S(1)} %reshape.145, pred[2]{0:T(512)(128)(4,1)S(1)} %fusion.31, s32[2]{0:T(128)S(1)} %bitcast.74, pred[8]{0:T(512)(128)(4,1)S(1)} %fusion.29), kind=kOutput, calls=%fused_computation.10 | convolution fusion | flops 16514592 | bytes 11929618 | tf_op jit(solution)/shard_map/bp,ptd->btd/dot_general | solution.py:67
  347.6 0.1 copy.68
  347.7 0.1 rsqrt.24
  347.8 10.4 %copy.69 = f32[8,64,3584]{2,1,0:T(8,128)} copy(f32[8,64,3584]{2,0,1:T(8,128)} %get-tuple-element.11) | data formatting | bytes 14680064 | tf_op jit(solution)/shard_map/convert_element_type | solution.py:81
  358.2 13.6 %reshape.151 = f32[512,8,4,112]{3,2,1,0:T(4,128)} reshape(f32[8,64,3584]{2,1,0:T(8,128)} %copy.69) | data formatting | bytes 14680064 | tf_op jit(solution)/shard_map/convert_element_type | solution.py:81
  371.8 6.8 %fusion.10 = bf16[512,4,8,112]{3,1,2,0:T(4,128)(2,1)} fusion(f32[512,8,4,112]{3,2,1,0:T(4,128)} %reshape.151, f32[8,4,112]{2,1,0:T(4,128)S(1)} %mul.173, f32[512]{0:T(512)S(1)} %rsqrt.24), kind=kLoop, calls=%fused_computation.20 | loop fusion | flops 5505024 | bytes 11026432 | tf_op jit(solution)/shard_map/transpose | solution.py:99
  378.6 7.3 %copy.71 = bf16[512,4,8,112]{0,3,2,1:T(8,128)(2,1)} copy(bf16[512,4,8,112]{3,1,2,0:T(4,128)(2,1)} %fusion.10) | data formatting | bytes 7340032 | tf_op jit(solution)/shard_map/transpose | solution.py:99
  386.0 5.9 %convolution_convert_fusion.1 = bf16[3584,512]{1,0:T(8,128)(2,1)} fusion(bf16[512,3584]{0,1:T(8,128)(2,1)} %bitcast.66, bf16[512,512]{1,0:T(8,128)(2,1)S(1)} %bitcast.70), kind=kOutput, calls=%fused_computation.16 | convolution fusion | flops 1880883200 | bytes 7864320 | tf_op jit(solution)/shard_map/dot_general | solution.py:103
  391.9 0.0 reduce-scatter.8.cloned.1.call-start
  391.9 0.2 fusion.24
  392.1 7.7 %fusion.5 = (f32[3584]{0:T(1024)S(1)}, f32[512]{0:T(512)S(1)}, f32[512,3584]{1,0:T(8,128)}) fusion(f32[8,64,3584]{2,1,0:T(8,128)} %copy.69, f32[512]{0:T(512)S(1)} %rsqrt.24, f32[3584]{0:T(1024)S(1)} %copy-done.1, bf16[512,512]{1,0:T(8,128)(2,1)S(1)} %fusion.24, bf16[3584,512]{1,0:T(8,128)(2,1)} %all-gather.8.cloned.1.call-done), kind=kOutput, calls=%fused_computation.9 | convolution fusion | flops 1890054144 | bytes 18907136 | tf_op jit(solution)/shard_map/dot_general | solution.py:84
  399.8 44.9 %all-reduce = (f32[512]{0:T(512)S(1)}, f32[3584]{0:T(1024)S(1)}) all-reduce(f32[512]{0:T(512)S(1)} %get-tuple-element.8, f32[3584]{0:T(1024)S(1)} %get-tuple-element.4), channel_id=1, replica_groups=mesh['node'=8,'local'=4] {'node','local'}, use_global_device_ids=true, to_apply=%region_11.12 | all-reduce | flops 4096 | bytes 32768 | tf_op jit(solution)/shard_map/psum | solution.py:113
  444.7 0.6 broadcast_multiply_fusion.1
  445.3 0.6 broadcast_multiply_fusion
  445.9 18.0 %reduce-scatter.6.cloned.1.call-done = bf16[896,512]{1,0:T(8,128)(2,1)} async-done(((bf16[3584,512]{1,0:T(8,128)(2,1)}), bf16[896,512]{1,0:T(8,128)(2,1)}) %reduce-scatter.6.cloned.1.call-update) | async-done | bytes 917520 | tf_op jit(solution)/shard_map/reduce_scatter | solution.py:102
  464.0 7.7 %fusion.2 = bf16[512,3584]{1,0:T(8,128)(2,1)} fusion(f32[8,64,3584]{2,1,0:T(8,128)} %copy.69, f32[512,3584]{1,0:T(8,128)} %get-tuple-element.12, f32[512]{0:T(512)S(1)} %broadcast_multiply_fusion.2, f32[512]{0:T(512)S(1)} %multiply_multiply_fusion.5, f32[3584]{0:T(1024)S(1)} %copy-done.1, f32[512]{0:T(512)S(1)} %rsqrt.24), kind=kLoop, calls=%fused_computation.6 | loop fusion | flops 11010048 | bytes 18370560 | tf_op jit(solution)/shard_map/convert_element_type | solution.py:114
  471.7 31.0 %reduce-scatter.8.cloned.1.call-done = bf16[112,512]{1,0:T(8,128)(2,1)} async-done(((bf16[896,512]{1,0:T(8,128)(2,1)}), bf16[112,512]{1,0:T(8,128)(2,1)}) %reduce-scatter.8.cloned.1.call-update) | async-done | bytes 114704 | tf_op jit(solution)/shard_map/reduce_scatter | solution.py:110
  502.7 1.6 convert_multiply_fusion
  (30 shorter events, 0.3 us)
Async XLA Ops:
  7.2 121.2 %all-gather.4.cloned.1.call-start = ((), (), s32[]{:S(2)}) async-start(), calls=%async_computation.5 | async-start | bytes 25804800 | tf_op jit(solution)/shard_map/all_gather | solution.py:43
  7.9 4.4 copy-start.2
  7.9 4.4 copy-start.3
  7.9 208.3 %reduce-scatter.4.cloned.1.call-start = ((), (), s32[]{:S(2)}) async-start(), calls=%async_computation.6 | async-start | bytes 4587520 | tf_op jit(solution)/shard_map/reduce_scatter | solution.py:47
  147.5 68.7 %copy-start.4 = (f32[3584]{0:T(1024)S(1)}, f32[3584]{0:T(1024)}, u32[]{:S(2)}) copy-start(f32[3584]{0:T(1024)} %param.21) | copy-start | bytes 43012
  147.6 147.1 %all-gather.6.cloned.1.call-start = ((), (), s32[]{:S(2)}) async-start(), calls=%async_computation.7 | async-start | bytes 4587520 | tf_op jit(solution)/shard_map/all_gather | solution.py:53
  222.1 170.0 %all-gather.8.cloned.1.call-start = ((), (), s32[]{:S(2)}) async-start(), calls=%async_computation.8 | async-start | bytes 3784704 | tf_op jit(solution)/shard_map/all_gather | solution.py:86
  302.6 5.3 %copy-start.5 = (s32[1,8,64]{2,1,0:T(8,128)S(1)}, s32[1,8,64]{2,1,0:T(8,128)}, u32[]{:S(2)}) copy-start(s32[1,8,64]{2,1,0:T(8,128)} %param.17) | copy-start | bytes 6148
  302.6 27.5 %copy-start.1 = (f32[3584]{0:T(1024)S(1)}, f32[3584]{0:T(1024)}, u32[]{:S(2)}) copy-start(f32[3584]{0:T(1024)} %param.26) | copy-start | bytes 43012
  302.6 27.6 %copy-start.6 = (s32[1,2]{1,0:T(1,128)S(1)}, s32[1,2]{1,0:T(1,128)}, u32[]{:S(2)}) copy-start(s32[1,2]{1,0:T(1,128)} %param.16) | copy-start | bytes 28
  302.6 27.7 %copy-start = (bf16[1,8,64,512]{3,2,1,0:T(8,128)(2,1)S(1)}, bf16[1,8,64,512]{3,2,1,0:T(8,128)(2,1)}, u32[]{:S(2)}) copy-start(bf16[1,8,64,512]{3,2,1,0:T(8,128)(2,1)} %param.19) | copy-start | bytes 1572868
  303.6 31.8 %all-to-all-start.1 = ((bf16[4,4,32,896]{3,2,0,1:T(8,128)(2,1)}), bf16[4,4,32,896]{3,2,0,1:T(8,128)(2,1)S(1)}, u32[]{:S(2)}, u32[]{:S(2)}) async-start(bf16[4,4,32,896]{3,2,0,1:T(8,128)(2,1)} %copy.64), calls=%async_computation.2 | async-start | bytes 1835008 | tf_op jit(solution)/shard_map/all_to_all | solution.py:61
  307.1 156.8 %reduce-scatter.6.cloned.1.call-start = ((), (), s32[]{:S(2)}) async-start(), calls=%async_computation.9 | async-start | bytes 4587520 | tf_op jit(solution)/shard_map/reduce_scatter | solution.py:102
  391.9 110.8 %reduce-scatter.8.cloned.1.call-start = ((), (), s32[]{:S(2)}) async-start(), calls=%async_computation.10 | async-start | bytes 1032192 | tf_op jit(solution)/shard_map/reduce_scatter | solution.py:110
Sparse Core Ops, SparseCore 0:
  9.9 118.4 all-gather.3
  147.7 68.5 reduce-scatter.3
  222.2 72.3 all-gather.5
  297.3 63.9 all-gather.7
  392.0 71.8 reduce-scatter.5
  467.0 35.6 reduce-scatter.7
where the time goes:
time: 512 us; the launch traced here: 511 us
  waiting for transfers between devices  220 us (43%)
  blocking collectives  146 us (29%)
  matrix products  52 us (10%)
  local copies, waits for them, and re-layouts  42.4 us (8%)
  other arithmetic  31.4 us (6%)
  between operations  14.9 us (3%)
    all_to_all x1, blocking collectives, per_device(): lax.all_to_all(normed, 'local', split_axis=1, concat_axis=0, tiled=True)  79.6 us
    all_gather x1, waiting for transfers between devices, per_device(): lax.all_gather(middle, 'local', axis=0, tiled=True)  71.2 us
    reduce_scatter x1, waiting for transfers between devices, per_device(): lax.psum_scatter(rounded.astype(jnp.float32).astype(jnp.bfloat16), 'local...  68.6 us
    psum x1, blocking collectives, per_device(): grad_bias, grad_gain = lax.psum((bias_part, gain_part), ('node', 'local'))  44.9 us
    reduce_scatter x1, waiting for transfers between devices, per_device(): lax.psum_scatter(partial_sum, 'node', scatter_dimension=0, tiled=True)  31 us
    all_gather x1, waiting for transfers between devices, per_device(): first_rows = lax.all_gather(proj_weight, 'node', axis=1, tiled=True)  25.3 us
    convert_element_type x2, local copies, waits for them, and re-layouts, per_device(): hidden_f = hidden.astype(jnp.float32)  24 us
    psum x1, blocking collectives, per_device(): doc_sizes = lax.psum(jnp.sum(doc_hits, 0), 'local')  21.8 us
  transfers between devices with their start and end apart: 7, of which 6 were waited for; matrix products, arithmetic and copies ran while one was open for 19% of the time, Pallas kernels for 0%

commit v1 on v0

v1 whole, which is shorter than its diff:
```python
import jax
import jax.numpy as jnp
from jax import lax
from jax.experimental import pallas as pl
from jax.experimental.pallas import tpu as pltpu
from jax.sharding import PartitionSpec as P

SLOTS = 2
DOCS = 16
CHUNKS = 2


def tail_kernel(
    piece_ref,
    text_ref,
    arrived_ref,
    grad_ref,
    weight_ref,
    gain_ref,
    out_ref,
    normed_ref,
    part_ref,
    hidden_ref,
):
    block = pl.program_id(0)
    is_image = piece_ref[block] >= 0

    @pl.when(is_image)
    def _():
        hidden_ref[...] = arrived_ref[0].astype(jnp.float32)

    @pl.when(jnp.logical_not(is_image))
    def _():
        hidden_ref[...] = text_ref[0].astype(jnp.float32)

    hidden_f = hidden_ref[...]
    inv_rms = lax.rsqrt(jnp.mean(hidden_f * hidden_f, -1, keepdims=True) + 1e-06)
    gain = gain_ref[...]
    unit = hidden_f * inv_rms
    normed_ref[0] = (unit * gain).astype(jnp.bfloat16)
    grad_normed = lax.dot_general(
        grad_ref[0], weight_ref[...], (((1,), (1,)), ((), ())), preferred_element_type=jnp.float32
    )
    part = jnp.sum(grad_normed * unit, 0, keepdims=True)

    @pl.when(block == 0)
    def _():
        part_ref[...] = part

    @pl.when(block > 0)
    def _():
        part_ref[...] += part

    scaled = grad_normed * gain
    hidden_f = hidden_ref[...]
    moment = jnp.mean(scaled * hidden_f, -1, keepdims=True)
    out_ref[0] = (
        inv_rms * scaled - hidden_f * (inv_rms * inv_rms * inv_rms * moment)
    ).astype(jnp.bfloat16)


def tail(piece_of_block, text, arrived, value_grad, v_full, norm_gain):
    blocks, rows, width = text.shape
    values = value_grad.shape[2]
    row_block = pl.BlockSpec((1, rows, width), lambda b, piece: (b, 0, 0))
    return pl.pallas_call(
        tail_kernel,
        grid_spec=pltpu.PrefetchScalarGridSpec(
            num_scalar_prefetch=1,
            grid=(blocks,),
            in_specs=[
                row_block,
                pl.BlockSpec((1, rows, width), lambda b, piece: (jnp.maximum(piece[b], 0), 0, 0)),
                pl.BlockSpec((1, rows, values), lambda b, piece: (b, 0, 0)),
                pl.BlockSpec((width, values), lambda b, piece: (0, 0)),
                pl.BlockSpec((1, width), lambda b, piece: (0, 0)),
            ],
            out_specs=[row_block, row_block, pl.BlockSpec((1, width), lambda b, piece: (0, 0))],
            scratch_shapes=[pltpu.VMEM((rows, width), jnp.float32)],
        ),
        out_shape=[
            jax.ShapeDtypeStruct((blocks, rows, width), jnp.bfloat16),
            jax.ShapeDtypeStruct((blocks, rows, width), jnp.bfloat16),
            jax.ShapeDtypeStruct((1, width), jnp.float32),
        ],
        cost_estimate=pl.CostEstimate(
            flops=2 * blocks * rows * width * values,
            bytes_accessed=8 * blocks * rows * width,
            transcendentals=0,
        ),
    )(piece_of_block, text, arrived, value_grad, v_full, norm_gain[None, :])


def layer_norm(vit_rows, scale_vec, shift_vec):
    values = vit_rows.astype(jnp.float32)
    average = jnp.mean(values, -1, keepdims=True)
    centred = values - average
    variance = jnp.mean(centred * centred, -1, keepdims=True)
    return (centred * lax.rsqrt(variance + 1e-05) * scale_vec + shift_vec).astype(jnp.bfloat16)


def per_device(
    vit_tiles,
    tile_counts,
    block_of_piece,
    segment_ids,
    text_rows,
    cotangent,
    proj_weight,
    proj_bias,
    out_weight,
    out_bias,
    ln_gain,
    ln_bias,
    norm_gain,
    v_weight,
):
    local_count = lax.axis_size("local")
    node_count = lax.axis_size("node")
    own_index = lax.axis_index("local")
    blocks = text_rows.shape[1]
    share_rows = text_rows.shape[2]
    model_width = text_rows.shape[3]
    out_cols = out_weight.shape[1]
    normed = layer_norm(vit_tiles[0, 0], ln_gain, ln_bias)
    received = lax.all_to_all(normed, "local", split_axis=1, concat_axis=0, tiled=True)
    bias_cols = lax.dynamic_slice_in_dim(out_bias, own_index * out_cols, out_cols, 0)
    v_full = lax.all_gather(
        lax.all_gather(v_weight, "local", axis=0, tiled=True), "node", axis=0, tiled=True
    )
    doc_ids = segment_ids[0].reshape(-1)
    doc_hits = (doc_ids[:, None] == lax.iota(jnp.int32, DOCS)[None, :]).astype(jnp.float32)
    doc_sizes = lax.psum(jnp.sum(doc_hits, 0), "local")
    doc_weight = blocks * share_rows * local_count / (DOCS * doc_sizes)
    token_weight = jnp.dot(doc_hits, doc_weight, precision=lax.Precision.HIGHEST)
    value_grad = (
        cotangent[0].reshape(-1, cotangent.shape[3]).astype(jnp.float32) * token_weight[:, None]
    ).astype(jnp.bfloat16)
    bias_part = jnp.sum(value_grad.astype(jnp.float32), 0)
    width_each = proj_weight.shape[1] // CHUNKS
    bias_chunks = proj_bias.reshape(node_count, CHUNKS, width_each)
    out_chunks = out_weight.reshape(node_count, CHUNKS, width_each, out_cols)
    out_chunks = [out_chunks[:, c].reshape(-1, out_cols) for c in range(CHUNKS)]
    gathered = [
        lax.all_gather(
            proj_weight[:, c * width_each : (c + 1) * width_each], "node", axis=1, tiled=True
        )
        for c in range(CHUNKS)
    ]
    sums = []
    for c in range(CHUNKS):
        term = jnp.dot(received, gathered[c], preferred_element_type=jnp.float32)
        rounded = lax.optimization_barrier(term.astype(jnp.bfloat16))
        sums.append(lax.psum_scatter(rounded, "local", scatter_dimension=0, tiled=True))
    sums[0], value_grad, bias_part, out_chunks = lax.optimization_barrier(
        (sums[0], value_grad, bias_part, out_chunks)
    )
    projected = bias_cols
    for c in range(CHUNKS):
        middle = jax.nn.gelu(
            sums[c].astype(jnp.float32) + bias_chunks[:, c].reshape(-1), approximate=False
        ).astype(jnp.bfloat16)
        projected = projected + jnp.dot(
            lax.all_gather(middle, "local", axis=0, tiled=True),
            out_chunks[c],
            preferred_element_type=jnp.float32,
        )
    columns_out = projected.astype(jnp.bfloat16)
    run_rows = share_rows // 2
    columns_out = columns_out.reshape(local_count, local_count, run_rows, out_cols)
    arrived = lax.all_to_all(columns_out, "local", split_axis=1, concat_axis=3, tiled=True)
    piece_total = local_count // 2
    arrived = arrived.reshape(piece_total, share_rows, model_width)
    piece_ids = lax.iota(jnp.int32, piece_total)
    filled = piece_ids % SLOTS < jnp.repeat(tile_counts[0], SLOTS)
    chosen = (block_of_piece[0][None, :] == lax.iota(jnp.int32, blocks)[:, None]) & filled[None, :]
    piece_of_block = jnp.max(jnp.where(chosen, piece_ids[None, :], -1), 1).astype(jnp.int32)
    grad_hidden, normed_input, gain_part = tail(
        piece_of_block,
        text_rows[0],
        arrived,
        value_grad.reshape(blocks, share_rows, -1),
        v_full,
        norm_gain,
    )
    partial_sum = lax.psum_scatter(
        lax.dot_general(
            normed_input.reshape(-1, model_width),
            value_grad,
            (((0,), (0,)), ((), ())),
            preferred_element_type=jnp.float32,
        ).astype(jnp.bfloat16),
        "node",
        scatter_dimension=0,
        tiled=True,
    )
    grad_bias, grad_gain = lax.psum((bias_part, gain_part[0]), ("node", "local"))
    partial_sum, grad_bias, grad_gain = lax.optimization_barrier(
        (partial_sum, grad_bias, grad_gain)
    )
    grad_weight = lax.psum_scatter(partial_sum, "local", scatter_dimension=0, tiled=True).astype(
        jnp.float32
    )
    grad_hidden = grad_hidden[None]
    return (grad_hidden, grad_weight / node_count, grad_bias / node_count, grad_gain / node_count)


def solution(mesh):
    in_specs = (
        P("node", "local", None, None),
        P("node", None),
        P("node", None),
        P("node", None, "local"),
        P("node", None, "local", None),
        P("node", None, "local", None),
        P("local", "node"),
        P(),
        P(None, "local"),
        P(),
        P(),
        P(),
        P(),
        P(("node", "local"), None),
    )
    out_specs = (P("node", None, "local", None), P(("node", "local"), None), P(), P())
    return jax.shard_map(
        per_device, mesh=mesh, in_specs=in_specs, out_specs=out_specs, check_vma=False
    )
```

time: 512 us -> 461 us (0.900)
  waiting for transfers between devices: 220 us -> 190 us
  local copies, waits for them, and re-layouts: 42.4 us -> 22 us
  Pallas kernels: 0 us -> 17.2 us
  matrix products: 52 us -> 39.4 us
  other arithmetic: 31.4 us -> 22.1 us
    reduce_scatter x3 -> x4, waiting for transfers between devices: 118 us -> 77.6 us  [the longest x2 46.4 us: per_device(): lax.psum_scatter(rounded, 'local', scatter_dimension=0, tiled=True)]
    convert_element_type x2 -> x0, local copies, waits for them, and re-layouts: 24 us -> none  [per_device(): hidden_f = hidden.astype(jnp.float32)]
    all_gather x0 -> x1, blocking collectives: none -> 19.3 us  [per_device(): lax.all_gather(v_weight, 'local', axis=0, tiled=True)]
    pallas_call x0 -> x1, Pallas kernels: none -> 17.2 us  [tail(): pl.pallas_call(tail_kernel, grid_spec=pltpu.PrefetchScalarGridSpec(num_sc...]
    all_to_all x1, waiting for transfers between devices: 4.93 us -> 20.9 us  [per_device(): lax.all_to_all(columns_out, 'local', split_axis=1, concat_axis=3, tiled=T...]
    all_gather x1 -> x2, waiting for transfers between devices: 71.2 us -> 57.8 us  [per_device(): lax.all_gather(middle, 'local', axis=0, tiled=True)]
    dot_general x5, matrix products: 51.8 us -> 39.2 us  [the longest x2 23.4 us: per_device(): term = jnp.dot(received, gathered[c], preferred_element_type=jnp.float32)]
    psum x1, blocking collectives: 21.8 us -> 12.3 us  [per_device(): doc_sizes = lax.psum(jnp.sum(doc_hits, 0), 'local')]
  transfers between devices with their start and end apart: 7 -> 10, of which waited for: 6 -> 9; matrix products, arithmetic and copies ran while one was open for 19% -> 16% of each run, Pallas kernels for 0% -> 0%
where the time goes in v1:
time: 461 us; the launch traced here: 460 us
  waiting for transfers between devices  190 us (41%)
  blocking collectives  151 us (33%)
  matrix products  39.4 us (9%)
  other arithmetic  22.1 us (5%)
  local copies, waits for them, and re-layouts  22 us (5%)
  Pallas kernels  17.2 us (4%)
  between operations  14.7 us (3%)
    all_to_all x1, blocking collectives, per_device(): lax.all_to_all(normed, 'local', split_axis=1, concat_axis=0, tiled=True)  79.6 us
    all_gather x2, waiting for transfers between devices, per_device(): lax.all_gather(middle, 'local', axis=0, tiled=True)  57.8 us
    reduce_scatter x2, waiting for transfers between devices, per_device(): lax.psum_scatter(rounded, 'local', scatter_dimension=0, tiled=True)  46.4 us
    psum x1, blocking collectives, per_device(): lax.psum((bias_part, gain_part[0]), ('node', 'local'))  39.5 us
    all_gather x2, waiting for transfers between devices, per_device(): lax.all_gather(proj_weight[:, c * width_each:(c + 1) * width_each], 'node...  31 us
    dot_general x2, matrix products, per_device(): term = jnp.dot(received, gathered[c], preferred_element_type=jnp.float32)  23.4 us
    reduce_scatter x1, waiting for transfers between devices, per_device(): lax.psum_scatter(partial_sum, 'local', scatter_dimension=0, tiled=True)  22.5 us
    all_to_all x1, waiting for transfers between devices, per_device(): lax.all_to_all(columns_out, 'local', split_axis=1, concat_axis=3, tiled=T...  20.9 us
  transfers between devices with their start and end apart: 10, of which 9 were waited for; matrix products, arithmetic and copies ran while one was open for 16% of the time, Pallas kernels for 0%

profile of v1, /device:TPU:0, one launch (start us, length us, event | category | flops | bytes accessed | tf_op | source)
XLA Modules:
  0.0 459.8 jit_solution(16715705876832412243)
XLA Ops:
  7.2 3.6 fusion.39
  10.9 0.7 all-gather.10.cloned.1.call-update
  11.7 4.3 copy.27
  16.0 1.7 convert_reduce_fusion
  17.8 1.7 fusion.1
  19.5 4.2 add_convert_fusion
  23.7 79.6 %all_to_all.31 = bf16[128,4,3200]{0,2,1:T(8,128)(2,1)S(1)} all-to-all(bf16[128,4,3200]{0,2,1:T(8,128)(2,1)S(1)} %add_convert_fusion), channel_id=1, replica_groups=mesh['node'=8,'local'=4] {'local'}, dimensions={1} | all-to-all | bytes 6553600 | tf_op jit(solution)/shard_map/all_to_all | solution.py:126
  103.3 3.4 copy.28
  106.7 12.4 %convolution_convert_fusion.2 = bf16[512,1792]{1,0:T(8,128)(2,1)} fusion(bf16[512,3200]{1,0:T(8,128)(2,1)} %bitcast.49, bf16[3200,1792]{0,1:T(8,128)(2,1)} %all-gather.6.cloned.1.call-done), kind=kOutput, calls=%fused_computation.7 | convolution fusion | flops 5872943104 | bytes 16580608 | tf_op jit(solution)/shard_map/dot_general | solution.py:152
  119.2 31.0 %all-gather.10.cloned.1.call-done = bf16[3200,1792]{0,1:T(8,128)(2,1)} async-done(((bf16[3200,224]{0,1:T(8,128)(2,1)}), bf16[3200,1792]{0,1:T(8,128)(2,1)}) %all-gather.10.cloned.1.call-update) | async-done | bytes 11468816 | tf_op jit(solution)/shard_map/all_gather | solution.py:145
  150.2 10.9 %convolution_convert_fusion.1 = bf16[512,1792]{1,0:T(8,128)(2,1)} fusion(bf16[512,3200]{1,0:T(8,128)(2,1)S(1)} %bitcast.50, bf16[3200,1792]{0,1:T(8,128)(2,1)} %all-gather.10.cloned.1.call-done), kind=kOutput, calls=%fused_computation.6 | convolution fusion | flops 5872943104 | bytes 16580608 | tf_op jit(solution)/shard_map/dot_general | solution.py:152
  161.2 0.1 eq.36
  161.3 0.1 convert_reduce_fusion.2
  161.4 12.3 %psum.21 = f32[16]{0:T(128)S(1)} all-reduce(f32[16]{0:T(128)S(1)} %convert_reduce_fusion.2), channel_id=1, replica_groups=mesh['node'=8,'local'=4] {'local'}, use_global_device_ids=true, to_apply=%region_5.0 | all-reduce | flops 16 | bytes 128 | tf_op jit(solution)/shard_map/psum | solution.py:133
  173.7 0.1 fusion.29
  173.8 0.1 mul.72
  173.9 0.1 reshape.98
  174.1 1.2 convert_reduce_fusion.1
  175.4 2.0 fusion.2
  177.4 5.1 %fusion.38 = (bf16[8,1,224,896]{3,2,1,0:T(8,128)(2,1)S(1)}, bf16[8,1,224,896]{3,2,1,0:T(8,128)(2,1)}) fusion(bf16[8,2,224,896]{3,2,1,0:T(8,128)(2,1)} %bitcast.46), kind=kLoop, calls=%fused_computation.78 | loop fusion | bytes 12845056 | tf_op jit(solution)/shard_map/slice | solution.py:143
  182.5 9.8 %reduce-scatter.5.cloned.1.call-done = bf16[128,1792]{1,0:T(8,128)(2,1)} async-done(((bf16[512,1792]{1,0:T(8,128)(2,1)}), bf16[128,1792]{1,0:T(8,128)(2,1)}) %reduce-scatter.5.cloned.1.call-update) | async-done | bytes 458768 | tf_op jit(solution)/shard_map/reduce_scatter | solution.py:154
  192.4 3.8 fusion.5
  196.2 0.2 all-gather.12.cloned.1.call-start
  196.5 36.6 %reduce-scatter.7.cloned.1.call-done = bf16[128,1792]{1,0:T(8,128)(2,1)} async-done(((bf16[512,1792]{1,0:T(8,128)(2,1)}), bf16[128,1792]{1,0:T(8,128)(2,1)}) %reduce-scatter.7.cloned.1.call-update) | async-done | bytes 458768 | tf_op jit(solution)/shard_map/reduce_scatter | solution.py:154
  233.1 3.8 fusion.8
  237.0 19.3 %all_gather.22 = bf16[448,512]{1,0:T(8,128)(2,1)} all-gather(bf16[112,512]{1,0:T(8,128)(2,1)S(1)} %copy-done.2), channel_id=1, replica_groups=mesh['node'=8,'local'=4] {'local'}, dimensions={0}, use_global_device_ids=true | all-gather | bytes 573440 | tf_op jit(solution)/shard_map/all_gather | solution.py:129
  256.3 0.8 dynamic_slice.3
  257.1 22.1 %all-gather.8.cloned.1.call-done = bf16[512,1792]{1,0:T(8,128)(2,1)} async-done(((bf16[128,1792]{1,0:T(8,128)(2,1)}), bf16[512,1792]{1,0:T(8,128)(2,1)}) %all-gather.8.cloned.1.call-update) | async-done | bytes 1835024 | tf_op jit(solution)/shard_map/all_gather | solution.py:164
  279.2 5.8 %fusion.40 = f32[512,896]{1,0:T(8,128)} fusion(bf16[512,1792]{1,0:T(8,128)(2,1)} %all-gather.8.cloned.1.call-done, bf16[1792,896]{1,0:T(8,128)(2,1)} %bitcast.52), kind=kOutput, calls=%fused_computation.80 | convolution fusion | flops 1644167168 | bytes 6881280 | tf_op jit(solution)/shard_map/dot_general | solution.py:163
  285.0 35.8 %all-gather.12.cloned.1.call-done = bf16[512,1792]{1,0:T(8,128)(2,1)} async-done(((bf16[128,1792]{1,0:T(8,128)(2,1)}), bf16[512,1792]{1,0:T(8,128)(2,1)}) %all-gather.12.cloned.1.call-update) | async-done | bytes 1835024 | tf_op jit(solution)/shard_map/all_gather | solution.py:164
  320.8 4.1 add_convert_fusion.1
  324.9 1.0 copy.29
  325.9 3.5 all-to-all-start.1
  329.5 0.6 broadcast_in_dim.14.gain_ref
  330.8 0.6 fusion.31.piece_ref
  331.4 20.9 %all-to-all-done.1 = bf16[4,4,32,896]{3,2,0,1:T(8,128)(2,1)S(1)} async-done(((bf16[4,4,32,896]{3,2,0,1:T(8,128)(2,1)}), bf16[4,4,32,896]{3,2,0,1:T(8,128)(2,1)S(1)}, u32[]{:S(2)}, u32[]{:S(2)}) %all-to-all-start.1) | async-done | bytes 917536 | tf_op jit(solution)/shard_map/all_to_all | solution.py:171
  352.3 0.7 copy.30
  353.1 1.3 reshape.100.arrived_ref
  354.3 1.6 all-gather.14.cloned.1.call-done.weight_ref
  355.9 17.2 %shard_map.165 = (bf16[8,64,3584]{2,1,0:T(8,128)(2,1)}, bf16[8,64,3584]{2,1,0:T(8,128)(2,1)}, f32[1,3584]{1,0:T(1,128)}) custom-call(s32[8]{0:T(128)} %fusion.31.piece_ref, bf16[8,64,3584]{2,1,0:T(8,128)(2,1)} %bitcast.48, bf16[2,64,3584]{2,1,0:T(8,128)(2,1)} %reshape.100.arrived_ref, bf16[8,64,512]{2,1,0:T(8,128)(2,1)} %bitcast.53, ...), custom_call_target="tpu_custom_call" | custom-call | flops 1879048192 | bytes 14680064 | tf_op jit(solution)/shard_map/pallas_call | solution.py:66
  373.1 5.9 %convolution_convert_fusion = bf16[3584,512]{1,0:T(8,128)(2,1)} fusion(bf16[512,3584]{1,0:T(8,128)(2,1)} %bitcast.58, bf16[512,512]{1,0:T(8,128)(2,1)S(1)} %copy-done.1), kind=kOutput, calls=%fused_computation.4 | convolution fusion | flops 1880883200 | bytes 7864320 | tf_op jit(solution)/shard_map/dot_general | solution.py:187
  379.1 0.6 copy-done.7
  379.8 39.5 %all-reduce = (f32[512]{0:T(512)S(1)}, f32[3584]{0:T(1024)S(1)}) all-reduce(f32[512]{0:T(512)S(1)} %convert_reduce_fusion.1, f32[3584]{0:T(1024)S(1)} %reduce.4), channel_id=1, replica_groups=mesh['node'=8,'local'=4] {'node','local'}, use_global_device_ids=true, to_apply=%region_9.10 | all-reduce | flops 4096 | bytes 32768 | tf_op jit(solution)/shard_map/psum | solution.py:197
  419.3 8.7 %reduce-scatter.9.cloned.1.call-done = bf16[448,512]{1,0:T(8,128)(2,1)} async-done(((bf16[3584,512]{1,0:T(8,128)(2,1)}), bf16[448,512]{1,0:T(8,128)(2,1)}) %reduce-scatter.9.cloned.1.call-update) | async-done | bytes 458768 | tf_op jit(solution)/shard_map/reduce_scatter | solution.py:186
  428.0 0.6 broadcast_multiply_fusion.1
  428.6 0.6 broadcast_multiply_fusion
  429.2 22.5 %reduce-scatter.11.cloned.1.call-done = bf16[112,512]{1,0:T(8,128)(2,1)} async-done(((bf16[448,512]{1,0:T(8,128)(2,1)}), bf16[112,512]{1,0:T(8,128)(2,1)}) %reduce-scatter.11.cloned.1.call-update) | async-done | bytes 114704 | tf_op jit(solution)/shard_map/reduce_scatter | solution.py:201
  451.7 1.6 convert_multiply_fusion
  (45 shorter events, 0.8 us)
Async XLA Ops:
  7.2 99.5 %all-gather.6.cloned.1.call-start = ((), (), s32[]{:S(2)}) async-start(), calls=%async_computation.6 | async-start | bytes 12902400 | tf_op jit(solution)/shard_map/all_gather | solution.py:145
  10.9 139.4 %all-gather.10.cloned.1.call-start = ((), (), s32[]{:S(2)}) async-start(), calls=%async_computation.9 | async-start | bytes 12902400 | tf_op jit(solution)/shard_map/all_gather | solution.py:145
  11.6 4.4 copy-start.3
  11.6 4.4 copy-start.4
  11.6 180.7 %reduce-scatter.5.cloned.1.call-start = ((), (), s32[]{:S(2)}) async-start(), calls=%async_computation.7 | async-start | bytes 2293760 | tf_op jit(solution)/shard_map/reduce_scatter | solution.py:154
  106.7 43.6 %copy-start = (bf16[4,128,3200]{2,1,0:T(8,128)(2,1)S(1)}, bf16[4,128,3200]{2,1,0:T(8,128)(2,1)}, u32[]{:S(2)}) copy-start(bf16[4,128,3200]{2,1,0:T(8,128)(2,1)} %copy.28) | copy-start | bytes 9830404
  119.1 42.1 %copy-start.8 = (s32[1,8,64]{2,1,0:T(8,128)S(1)}, s32[1,8,64]{2,1,0:T(8,128)}, u32[]{:S(2)}) copy-start(s32[1,8,64]{2,1,0:T(8,128)} %param.17) | copy-start | bytes 6148
  119.1 54.8 %copy-start.5 = (f32[3584]{0:T(1024)S(1)}, f32[3584]{0:T(1024)}, u32[]{:S(2)}) copy-start(f32[3584]{0:T(1024)} %param.21) | copy-start | bytes 43012
  119.1 113.9 %reduce-scatter.7.cloned.1.call-start = ((), (), s32[]{:S(2)}) async-start(), calls=%async_computation.10 | async-start | bytes 2293760 | tf_op jit(solution)/shard_map/reduce_scatter | solution.py:154
  161.2 118.0 %all-gather.8.cloned.1.call-start = ((), (), s32[]{:S(2)}) async-start(), calls=%async_computation.8 | async-start | bytes 2293760 | tf_op jit(solution)/shard_map/all_gather | solution.py:164
  177.4 59.6 %copy-start.2 = (bf16[112,512]{1,0:T(8,128)(2,1)S(1)}, bf16[112,512]{1,0:T(8,128)(2,1)}, u32[]{:S(2)}) copy-start(bf16[112,512]{1,0:T(8,128)(2,1)} %param.27) | copy-start | bytes 344068
  196.2 124.6 %all-gather.12.cloned.1.call-start = ((), (), s32[]{:S(2)}) async-start(), calls=%async_computation.11 | async-start | bytes 2293760 | tf_op jit(solution)/shard_map/all_gather | solution.py:164
  236.9 119.0 %all-gather.14.cloned.1.call-start = ((), (), s32[]{:S(2)}) async-start(), calls=%async_computation.12 | async-start | bytes 4128768 | tf_op jit(solution)/shard_map/all_gather | solution.py:128
  324.9 4.6 %copy-start.6 = (f32[3584]{0:T(1024)S(1)}, f32[3584]{0:T(1024)}, u32[]{:S(2)}) copy-start(f32[3584]{0:T(1024)} %param.26) | copy-start | bytes 43012
  324.9 5.9 %copy-start.9 = (s32[1,2]{1,0:T(1,128)S(1)}, s32[1,2]{1,0:T(1,128)}, u32[]{:S(2)}) copy-start(s32[1,2]{1,0:T(1,128)} %param.16) | copy-start | bytes 28
  325.9 26.4 %all-to-all-start.1 = ((bf16[4,4,32,896]{3,2,0,1:T(8,128)(2,1)}), bf16[4,4,32,896]{3,2,0,1:T(8,128)(2,1)S(1)}, u32[]{:S(2)}, u32[]{:S(2)}) async-start(bf16[4,4,32,896]{3,2,0,1:T(8,128)(2,1)} %copy.29), calls=%async_computation.3 | async-start | bytes 1835008 | tf_op jit(solution)/shard_map/all_to_all | solution.py:171
  329.5 98.5 %reduce-scatter.9.cloned.1.call-start = ((), (), s32[]{:S(2)}) async-start(), calls=%async_computation.13 | async-start | bytes 4128768 | tf_op jit(solution)/shard_map/reduce_scatter | solution.py:186
  355.9 17.2 %copy-start.1 = (bf16[512,512]{1,0:T(8,128)(2,1)S(1)}, bf16[512,512]{1,0:T(8,128)(2,1)}, u32[]{:S(2)}) copy-start(bf16[512,512]{1,0:T(8,128)(2,1)} %fusion.2) | copy-start | bytes 1572868
  379.1 0.7 copy-start.7
  379.1 72.6 %reduce-scatter.11.cloned.1.call-start = ((), (), s32[]{:S(2)}) async-start(), calls=%async_computation.14 | async-start | bytes 573440 | tf_op jit(solution)/shard_map/reduce_scatter | solution.py:201
Sparse Core Ops, SparseCore 0:
  11.0 69.9 all-gather.5
  82.9 67.2 all-gather.9
  152.5 39.7 reduce-scatter.4
  194.5 38.5 reduce-scatter.6
  234.5 44.6 all-gather.7
  280.6 40.1 all-gather.11
  322.7 33.1 all-gather.13
  379.2 48.7 reduce-scatter.8
  430.3 21.3 reduce-scatter.10
